TPU v7x, 32 devices: a whole 2x2x4 slice. The times are simulated.
32 devices in a mesh: groups: 2 (over x), attn: 4 (over y, core), expert: 4 (over z).
Axes of the slice: x: 2, y: 2, z: 4, core: 2. Of those that a mesh axis runs over, the one named last changes fastest.
Arguments:
- tokens: bfloat16 [1024, 4096], P(('groups', 'attn'), 'expert'), parts along dimension 0, may hold values from -6 to 6
- expert_ids: int32 [1024, 8], P(('groups', 'attn')), parts along dimension 0, may hold values from 0 to 15, all different within a row; in each aligned block of 128 rows (0 to 127, 128 to 255, ...) at most 128 rows name the same one
- gate_weight: bfloat16 [1024, 8], P(('groups', 'attn')), parts along dimension 0, may hold values from 0.049804688 to 0.29882812
- w_gate: bfloat16 [16, 4096, 768], P('attn', 'expert'), may hold values from -0.09375 to 0.09375
- w_up: bfloat16 [16, 4096, 768], P('attn', 'expert'), may hold values from -0.09375 to 0.09375
- w_down: bfloat16 [16, 768, 4096], P('attn', None, 'expert'), may hold values from -0.21875 to 0.21875
- query: bfloat16 [64, 64, 128], P(('groups', 'attn', 'expert')), parts along dimension 0, may hold values from -100 to 100
- cache_k: bfloat16 [64, 768, 4, 128], P(('groups', 'attn', 'expert')), parts along dimension 0, may hold values from -6 to 6
- cache_v: bfloat16 [64, 768, 4, 128], P(('groups', 'attn', 'expert')), parts along dimension 0, may hold values from -6 to 6
- lengths: int32 [64], P(('groups', 'attn', 'expert')), parts along dimension 0, may hold values from 2 to 768, as said below
Outputs:
- moe_out: bfloat16 [1024, 4096], P(('groups', 'attn'), 'expert'), parts along dimension 0
- attn_out: bfloat16 [64, 8192], P(('groups', 'attn', 'expert')), parts along dimension 0
There are 2 independent parts, one for each index of `groups`. A program takes and returns all parts, laid end to end along the dimension named above; an argument that names none is the same for every part. Nothing has to cross between parts.
Inputs may be any that keep to these rules, and one draw needn't show every extreme that they name: `expert_ids`: each row names 8 different experts. In the rows of one index of attn (aligned blocks of 128 rows) no expert is named by more than 128 rows, and in some block some expert by exactly 128. `lengths`: some sequence has all 768 positions live.
All inputs are finite; a program needn't handle non-finite values.
Results may differ from a plain program's by a relative error of at most 0.025.
Values may be sent and summed in bfloat16 or wider, within the bound.
A program may use at most 64 MiB of HBM per device.

v0:
```python
import jax
import jax.numpy as jnp
from jax import lax
from jax.sharding import PartitionSpec as P


def member_table(expert_ids, experts):
    wanted = jnp.arange(experts, dtype=jnp.int32)
    return jnp.any(expert_ids[:, :, None] == wanted[None, None, :], axis=1).astype(jnp.int32)


def pad_rows(values):
    feat_width = values.shape[-1]
    flat_rows = values.reshape(-1, feat_width)
    return jnp.concatenate([flat_rows, jnp.zeros((1, feat_width), values.dtype)], axis=0)


def return_slots(results, starts_in, kept_in, slot_count):
    local_experts = results.shape[0]
    capacity = results.shape[1]
    slot_ids = jnp.arange(slot_count, dtype=jnp.int32)[None, None, :]
    column = jnp.arange(local_experts, dtype=jnp.int32)[None, :, None]
    row_index = column * capacity + starts_in[:, :, None] + slot_ids
    row_index = jnp.where(slot_ids < kept_in[:, :, None], row_index, local_experts * capacity)
    return pad_rows(results)[row_index]


def grouped_attention(query, cache_k, cache_v, lengths):
    seq_count, head_total, head_size = query.shape
    context = cache_k.shape[1]
    kv_count = cache_k.shape[2]
    grouped = query.reshape(seq_count, kv_count, head_total // kv_count, head_size)
    scores = jnp.einsum(
        "skgd,slkd->skgl", grouped, cache_k, preferred_element_type=jnp.float32
    ) * head_size ** (-0.5)
    live_mask = (
        lax.broadcasted_iota(jnp.int32, (seq_count, 1, 1, context), 3)
        < lengths[:, None, None, None]
    )
    masked = jnp.where(live_mask, scores, -jnp.inf)
    row_peak = jnp.max(masked, axis=3, keepdims=True)
    weighted = jnp.exp(masked - row_peak)
    denominator = jnp.sum(weighted, axis=3, keepdims=True)
    prob_bf = (weighted / denominator).astype(jnp.bfloat16)
    attended = jnp.einsum("skgl,slkd->skgd", prob_bf, cache_v, preferred_element_type=jnp.float32)
    return attended.reshape(seq_count, head_total * head_size).astype(jnp.bfloat16)


def body(tokens, expert_ids, gate_weight, w_gate, w_up, w_down, query, cache_k, cache_v, lengths):
    tok_rows, feat_width = tokens.shape
    top_count = expert_ids.shape[1]
    local_experts = w_gate.shape[0]
    ffn_width = w_gate.shape[2]
    attn_count = lax.axis_size("attn")
    experts = local_experts * attn_count
    capacity = tok_rows * top_count // local_experts
    slot_count = min(tok_rows, 3 * tok_rows * top_count // experts)
    member = member_table(expert_ids, experts)
    local_rank = jnp.cumsum(member, axis=0, dtype=jnp.int32) - member
    whole_ids = None
    whole_tokens, whole_ids, whole_gates = (
        lax.all_gather(tokens, "attn", axis=0, tiled=True),
        lax.all_gather(expert_ids, "attn", axis=0, tiled=True),
        lax.all_gather(gate_weight, "attn", axis=0, tiled=True),
    )
    all_rows = whole_tokens.shape[0]
    whole_member = member_table(whole_ids, experts)
    all_counts = jnp.sum(
        whole_member.reshape(attn_count, tok_rows, experts), axis=1, dtype=jnp.int32
    )
    src_offsets = jnp.cumsum(all_counts, axis=0, dtype=jnp.int32) - all_counts
    src_kept = jnp.clip(capacity - src_offsets, 0, all_counts)
    my_index = lax.axis_index("attn")
    offsets = lax.dynamic_index_in_dim(src_offsets, my_index, 0, keepdims=False)
    position = offsets[None, :] + local_rank
    starts_in = lax.dynamic_slice_in_dim(src_offsets, my_index * local_experts, local_experts, 1)
    kept_in = lax.dynamic_slice_in_dim(src_kept, my_index * local_experts, local_experts, 1)
    my_member = lax.dynamic_slice_in_dim(whole_member, my_index * local_experts, local_experts, 1)
    queue_place = jnp.cumsum(my_member, axis=0, dtype=jnp.int32) - my_member
    pack_target = jnp.where(
        (my_member > 0) & (queue_place < capacity),
        jnp.arange(local_experts, dtype=jnp.int32)[None, :] * capacity + queue_place,
        local_experts * capacity,
    )
    holders = jnp.broadcast_to(
        jnp.arange(all_rows, dtype=jnp.int32)[:, None], (all_rows, local_experts)
    )
    pack_index = (
        jnp.full((local_experts * capacity,), all_rows, jnp.int32)
        .at[pack_target.reshape(-1)]
        .set(holders.reshape(-1), mode="drop")
    )
    packed = pad_rows(whole_tokens)[pack_index].reshape(local_experts, capacity, feat_width)
    gate_part = jnp.einsum("jrd,jdf->jrf", packed, w_gate, preferred_element_type=jnp.float32)
    up_part = jnp.einsum("jrd,jdf->jrf", packed, w_up, preferred_element_type=jnp.float32)
    both_parts = jnp.concatenate([gate_part, up_part], axis=2)
    both_sums = lax.psum(both_parts.astype(jnp.bfloat16), "expert").astype(jnp.float32)
    hidden = (jax.nn.silu(both_sums[:, :, :ffn_width]) * both_sums[:, :, ffn_width:]).astype(
        jnp.bfloat16
    )
    results = jnp.einsum("jrf,jfd->jrd", hidden, w_down, preferred_element_type=jnp.float32).astype(
        jnp.bfloat16
    )
    back_rows = return_slots(results, starts_in, kept_in, slot_count)
    returned = lax.all_to_all(back_rows, "attn", split_axis=0, concat_axis=0, tiled=True)
    slot_of = jnp.take_along_axis(local_rank, expert_ids, axis=1)
    place_of = jnp.take_along_axis(position, expert_ids, axis=1)
    keep_mask = place_of < capacity
    picked = returned.reshape(experts * slot_count, feat_width)[expert_ids * slot_count + slot_of]
    factor = jnp.where(keep_mask, gate_weight.astype(jnp.float32), 0.0)
    moe_out = jnp.sum(factor[:, :, None] * picked.astype(jnp.float32), axis=1).astype(jnp.bfloat16)
    attn_out = grouped_attention(query, cache_k, cache_v, lengths)
    return (moe_out, attn_out)


def solution(mesh):
    return jax.shard_map(
        body,
        mesh=mesh,
        in_specs=(
            P(("groups", "attn"), "expert"),
            P(("groups", "attn"), None),
            P(("groups", "attn"), None),
            P("attn", "expert", None),
            P("attn", "expert", None),
            P("attn", None, "expert"),
            P(("groups", "attn", "expert"), None, None),
            P(("groups", "attn", "expert"), None, None, None),
            P(("groups", "attn", "expert"), None, None, None),
            P(("groups", "attn", "expert")),
        ),
        out_specs=(P(("groups", "attn"), "expert"), P(("groups", "attn", "expert"), None)),
        check_vma=False,
    )
```

profile of v0, /device:TPU:0, one launch (start us, length us, event | category | flops | bytes accessed | tf_op | source)
XLA Modules:
  0.0 263.3 jit_solution(12744865341679624601)
XLA Ops:
  7.2 0.0 copy-start
  7.2 0.0 all-gather.2.cloned.1.call-start
  7.2 0.7 all-gather.2.cloned.1.call-update
  7.9 0.0 all-reduce.4.cloned.1.call-start
  8.0 6.4 %all_gather.6 = s32[512,8]{0,1:T(8,128)S(1)} all-gather(s32[128,8]{0,1:T(8,128)} %param.13), channel_id=1, replica_groups=mesh['groups'=2,'attn'=4,'expert'=4] {'attn'}, dimensions={0}, use_global_device_ids=true | all-gather | bytes 20480 | tf_op jit(solution)/shard_map/all_gather | solution.py:63
  14.5 1.2 reduce-window.6
  15.7 0.2 slice_reduce_fusion
  15.9 0.2 reduce-window.9
  16.1 0.1 add_bitcast_fusion
  16.2 0.1 add_select_fusion
  16.2 0.1 copy.103
  16.4 0.2 reshape.138
  16.6 0.2 reshape.186
  16.8 8.0 %scatter_custom_fusion = s32[1024]{0:T(1024)S(1)} fusion(s32[2048]{0:T(1024)S(1)} %bitcast.56, s32[2048]{0:T(1024)S(1)} %reshape.186, s32[]{:T(128)} %constant.34.clone.1), kind=kCustom, calls=%fused_computation.57 | custom fusion | bytes 4100 | tf_op jit(solution)/shard_map/scatter | solution.py:91
  24.9 4.2 %all-gather.2.cloned.1.call-done = bf16[512,1024]{1,0:T(8,128)(2,1)} async-done(((bf16[128,1024]{1,0:T(8,128)(2,1)}), bf16[512,1024]{1,0:T(8,128)(2,1)}) %all-gather.2.cloned.1.call-update) | async-done | bytes 1048592 | tf_op jit(solution)/shard_map/all_gather | solution.py:62
  29.0 1.3 concatenate.10
  30.3 5.4 %gather_fusion = bf16[1024,1024]{1,0:T(8,128)(2,1)} fusion(bf16[513,1024]{1,0:T(8,128)(2,1)S(1)} %concatenate.10, s32[1024]{0:T(1024)S(1)} %fusion.24), kind=kCustom, calls=%fused_computation.2 | custom fusion | bytes 4198400 | tf_op jit(solution)/shard_map/gather | solution.py:93
  35.7 0.0 copy-start.1
  35.7 5.4 %convolution_convert_fusion.1 = bf16[4,256,768]{2,1,0:T(8,128)(2,1)S(1)} fusion(bf16[4,256,1024]{2,1,0:T(8,128)(2,1)} %bitcast.48, bf16[4,1024,768]{2,1,0:T(8,128)(2,1)} %param.16), kind=kOutput, calls=%fused_computation.13 | convolution fusion | flops 1611399168 | bytes 9961472 | tf_op jit(solution)/shard_map/jrd,jdf->jrf/dot_general | solution.py:95
  41.0 0.0 copy-done.1
  41.0 4.6 %convolution_convert_fusion.2 = bf16[4,256,768]{2,1,0:T(8,128)(2,1)S(1)} fusion(bf16[4,256,1024]{2,1,0:T(8,128)(2,1)S(1)} %bitcast.49, bf16[4,1024,768]{2,1,0:T(8,128)(2,1)} %param.15), kind=kOutput, calls=%fused_computation.14 | convolution fusion | flops 1611399168 | bytes 9961472 | tf_op jit(solution)/shard_map/jrd,jdf->jrf/dot_general | solution.py:94
  45.6 2.0 pad_maximum_fusion
  47.6 0.0 all-reduce.4.cloned.1.call-update
  47.6 0.3 reduce_sum.27
  48.0 0.2 reduce_window_sum.37
  48.2 0.1 dynamic-slice_minimum_fusion
  48.2 0.1 copy.104
  48.3 0.1 copy.105
  48.4 0.1 compare_select_fusion.1
  48.5 120.3 %all-reduce.4.cloned.1.call-done = bf16[4,256,1536]{2,1,0:T(8,128)(2,1)} async-done(((bf16[4,256,1536]{2,1,0:T(8,128)(2,1)}), bf16[4,256,1536]{2,1,0:T(8,128)(2,1)}) %all-reduce.4.cloned.1.call-update) | async-done | bytes 3145744 | tf_op jit(solution)/shard_map/psum | solution.py:97
  168.8 2.7 %convert_element_type.45 = f32[4,256,1536]{2,1,0:T(8,128)S(1)} convert(bf16[4,256,1536]{2,1,0:T(8,128)(2,1)} %all-reduce.4.cloned.1.call-done) | non-fusion elementwise | flops 1572864 | bytes 9437184 | tf_op jit(solution)/shard_map/convert_element_type | solution.py:97
  171.6 4.9 %convolution_convert_fusion = bf16[4,256,1024]{2,1,0:T(8,128)(2,1)S(1)} fusion(bf16[4,768,1024]{2,1,0:T(8,128)(2,1)} %param.17, f32[4,256,1536]{2,1,0:T(8,128)S(1)} %convert_element_type.45), kind=kOutput, calls=%fused_computation.12 | convolution fusion | flops 1616379904 | bytes 14680064 | tf_op jit(solution)/shard_map/jrf,jfd->jrd/dot_general | solution.py:101
  176.4 1.5 concatenate.12
  178.0 12.9 %gather_fusion.1 = bf16[2048,1024]{1,0:T(8,128)(2,1)} fusion(bf16[1025,1024]{1,0:T(8,128)(2,1)} %concatenate.12, s32[2048]{0:T(1024)S(1)} %broadcast_clamp_fusion), kind=kCustom, calls=%fused_computation.3 | custom fusion | bytes 8396800 | tf_op jit(solution)/shard_map/gather | solution.py:25
  190.8 0.0 copy-start.2
  190.8 5.2 %all-to-all-start = ((bf16[4,4,128,1024]{3,2,1,0:T(8,128)(2,1)}), bf16[4,4,128,1024]{3,2,1,0:T(8,128)(2,1)}, u32[]{:S(2)}, u32[]{:S(2)}) async-start(bf16[4,4,128,1024]{3,2,1,0:T(8,128)(2,1)} %bitcast.47), calls=%async_computation | async-start | bytes 8388608 | tf_op jit(solution)/shard_map/all_to_all | solution.py:105
  196.0 0.0 copy-done.2
  196.0 0.1 copy.99
  196.2 0.2 reduce_window_sum.38
  196.3 0.1 copy.100
  196.4 0.1 reshape.206
  196.5 0.2 dynamic-slice_reduce_fusion
  196.7 7.1 %gather_fusion.4 = s32[1024]{0:T(1024)S(1)} fusion(s32[128,16]{1,0:T(8,128)S(1)} %get-tuple-element.4, s32[1024]{0:T(1024)S(1)} %reshape.206), kind=kCustom, calls=%fused_computation.1.clone | custom fusion | bytes 16384 | tf_op jit(solution)/shard_map/jit(take_along_axis)/gather | solution.py:106
  203.8 0.1 reshape.214
  204.0 0.1 copy.108
  204.1 0.1 reshape.176
  204.2 0.0 copy-start.4
  204.2 0.0 copy-start.5
  204.2 0.0 copy-start.3
  204.2 7.1 %gather_fusion.3 = s32[1024]{0:T(1024)S(1)} fusion(s32[128,16]{1,0:T(8,128)S(1)} %get-tuple-element.3, s32[1024]{0:T(1024)S(1)} %reshape.206), kind=kCustom, calls=%fused_computation.clone | custom fusion | bytes 16384 | tf_op jit(solution)/shard_map/jit(take_along_axis)/gather | solution.py:107
  211.3 0.1 reshape.209
  211.4 0.0 copy-done.4
  211.5 0.1 copy.102
  211.6 0.0 copy-done.5
  211.6 0.1 iota_compare_fusion.3
  211.7 0.0 copy-done
  211.7 0.0 copy-done.3
  211.7 0.5 fusion.14
  212.2 0.2 fusion.29
  212.4 1.8 fusion.17
  214.2 0.7 copy.127
  214.9 29.1 %all-to-all-done = bf16[4,4,128,1024]{3,2,1,0:T(8,128)(2,1)} async-done(((bf16[4,4,128,1024]{3,2,1,0:T(8,128)(2,1)}), bf16[4,4,128,1024]{3,2,1,0:T(8,128)(2,1)}, u32[]{:S(2)}, u32[]{:S(2)}) %all-to-all-start) | async-done | bytes 4194336 | tf_op jit(solution)/shard_map/all_to_all | solution.py:105
  244.0 8.8 %gather_fusion.2 = bf16[1024,1024]{1,0:T(8,128)(2,1)} fusion(bf16[2048,1024]{1,0:T(8,128)(2,1)} %bitcast.8, s32[1024]{0:T(1024)S(1)} %broadcast_clamp_fusion.1), kind=kCustom, calls=%fused_computation.4 | custom fusion | bytes 4198400 | tf_op jit(solution)/shard_map/gather | solution.py:109
  252.8 3.7 %fusion.1 = bf16[128,1024]{1,0:T(8,128)(2,1)} fusion(bf16[1024,1024]{1,0:T(8,128)(2,1)} %gather_fusion.2, f32[128,8]{1,0:T(8,128)S(1)} %copy.102), kind=kLoop, calls=%fused_computation.8 | loop fusion | flops 3014656 | bytes 2363392 | tf_op jit(solution)/shard_map/reduce_sum | solution.py:111
  (20 shorter events, 0.3 us)
Async XLA Ops:
  7.2 204.5 %copy-start = (bf16[2,768,4,128]{3,2,1,0:T(4,128)(2,1)S(1)}, bf16[2,768,4,128]{3,2,1,0:T(4,128)(2,1)}, u32[]{:S(2)}) copy-start(bf16[2,768,4,128]{3,2,1,0:T(4,128)(2,1)} %param.19) | copy-start | bytes 4718596
  7.2 21.8 %all-gather.2.cloned.1.call-start = ((), (), s32[]{:S(2)}) async-start(), calls=%async_computation.1 | async-start | bytes 1310720 | tf_op jit(solution)/shard_map/all_gather | solution.py:62
  7.9 160.9 %all-reduce.4.cloned.1.call-start = ((), (), s32[]{:S(2)}) async-start(), calls=%async_computation.2 | async-start | bytes 6291456 | tf_op jit(solution)/shard_map/psum | solution.py:97
  35.7 5.4 %copy-start.1 = (bf16[1024,1024]{1,0:T(8,128)(2,1)S(1)}, bf16[1024,1024]{1,0:T(8,128)(2,1)}, u32[]{:S(2)}) copy-start(bf16[1024,1024]{1,0:T(8,128)(2,1)} %gather_fusion) | copy-start | bytes 6291460
  190.8 5.2 %copy-start.2 = (s32[128,8]{0,1:T(8,128)S(1)}, s32[128,8]{0,1:T(8,128)}, u32[]{:S(2)}) copy-start(s32[128,8]{0,1:T(8,128)} %param.13) | copy-start | bytes 12292
  190.8 53.2 %all-to-all-start = ((bf16[4,4,128,1024]{3,2,1,0:T(8,128)(2,1)}), bf16[4,4,128,1024]{3,2,1,0:T(8,128)(2,1)}, u32[]{:S(2)}, u32[]{:S(2)}) async-start(bf16[4,4,128,1024]{3,2,1,0:T(8,128)(2,1)} %bitcast.47), calls=%async_computation | async-start | bytes 8388608 | tf_op jit(solution)/shard_map/all_to_all | solution.py:105
  204.2 7.3 %copy-start.4 = (bf16[128,8]{0,1:T(8,128)(2,1)S(1)}, bf16[128,8]{0,1:T(8,128)(2,1)}, u32[]{:S(2)}) copy-start(bf16[128,8]{0,1:T(8,128)(2,1)} %param.14) | copy-start | bytes 6148
  204.2 7.4 %copy-start.5 = (s32[2]{0:T(128)S(1)}, s32[2]{0:T(128)}, u32[]{:S(2)}) copy-start(s32[2]{0:T(128)} %param.21) | copy-start | bytes 28
  204.2 7.4 %copy-start.3 = (bf16[2,64,128]{2,1,0:T(8,128)(2,1)S(1)}, bf16[2,64,128]{2,1,0:T(8,128)(2,1)}, u32[]{:S(2)}) copy-start(bf16[2,64,128]{2,1,0:T(8,128)(2,1)} %param.18) | copy-start | bytes 98308
Sparse Core Ops, SparseCore 0:
  9.5 19.4 all-gather.1
  47.7 121.0 all-reduce.3
where the time goes:
time: 264 us; the launch traced here: 263 us
  waiting for transfers between devices  154 us (58%)
  local copies, waits for them, and re-layouts  54.7 us (21%)
  matrix products  17.1 us (6%)
  between operations  14.3 us (5%)
  other arithmetic  11.2 us (4%)
  blocking collectives  6.41 us (2%)
  starting transfers between devices  5.25 us (2%)
    psum x1, waiting for transfers between devices, body(): lax.psum(both_parts.astype(jnp.bfloat16), 'expert').astype(jnp.float32)  120 us
    all_to_all x1, waiting for transfers between devices, body(): lax.all_to_all(back_rows, 'attn', split_axis=0, concat_axis=0, tiled=True)  29.1 us
    gather x1, local copies, waits for them, and re-layouts, return_slots(): return pad_rows(results)[row_index]  12.9 us
    gather x1, local copies, waits for them, and re-layouts, body(): returned.reshape(experts * slot_count, feat_width)  8.78 us
    scatter x1, local copies, waits for them, and re-layouts, body(): pack_index = jnp.full((local_experts * capacity,), all_rows, jnp.int32).a...  8.04 us
    gather x5, local copies, waits for them, and re-layouts, body(): place_of = jnp.take_along_axis(position, expert_ids, axis=1)  7.39 us
    gather x3, local copies, waits for them, and re-layouts, body(): slot_of = jnp.take_along_axis(local_rank, expert_ids, axis=1)  7.2 us
    all_gather x1, blocking collectives, body(): lax.all_gather(expert_ids, 'attn', axis=0, tiled=True)  6.41 us
  transfers between devices with their start and end apart: 3, of which 3 were waited for; matrix products, arithmetic and copies ran while one was open for 11% of the time, Pallas kernels for 0%

commit v1 on v0

--- a/solution.py
+++ b/solution.py
@@ -94,7 +94,9 @@
     gate_part = jnp.einsum("jrd,jdf->jrf", packed, w_gate, preferred_element_type=jnp.float32)
     up_part = jnp.einsum("jrd,jdf->jrf", packed, w_up, preferred_element_type=jnp.float32)
     both_parts = jnp.concatenate([gate_part, up_part], axis=2)
-    both_sums = lax.psum(both_parts.astype(jnp.bfloat16), "expert").astype(jnp.float32)
+    both_sums = jnp.sum(lax.all_gather(both_parts.astype(jnp.bfloat16), "expert"), axis=0).astype(
+        jnp.float32
+    )
     hidden = (jax.nn.silu(both_sums[:, :, :ffn_width]) * both_sums[:, :, ffn_width:]).astype(
         jnp.bfloat16
     )

time: 264 us -> 370 us (1.40)
  waiting for transfers between devices: 154 us -> 251 us
  other arithmetic: 11.2 us -> 20.3 us
    all_gather x0 -> x1, waiting for transfers between devices: none -> 217 us  [body(): lax.all_gather(both_parts.astype(jnp.bfloat16), 'expert')]
    psum x1 -> x0, waiting for transfers between devices: 120 us -> none  [body(): lax.psum(both_parts.astype(jnp.bfloat16), 'expert').astype(jnp.float32)]
    reduce_sum x0 -> x1, other arithmetic: none -> 9.15 us  [body(): jnp.sum(lax.all_gather(both_parts.astype(jnp.bfloat16), 'expert'), axis=0)]
  transfers between devices with their start and end apart: 3 -> 3, of which waited for: 3 -> 3; matrix products, arithmetic and copies ran while one was open for 11% -> 8% of each run, Pallas kernels for 0% -> 0%
where the time goes in v1:
time: 370 us
  waiting for transfers between devices  251 us (68%)
  local copies, waits for them, and re-layouts  54.7 us (15%)
  other arithmetic  20.3 us (5%)
  matrix products  17.1 us (5%)
  between operations  14.3 us (4%)
  blocking collectives  6.41 us (2%)
  starting transfers between devices  5.25 us (1%)
    all_gather x1, waiting for transfers between devices, body(): lax.all_gather(both_parts.astype(jnp.bfloat16), 'expert')  217 us
    all_to_all x1, waiting for transfers between devices, body(): lax.all_to_all(back_rows, 'attn', split_axis=0, concat_axis=0, tiled=True)  29.1 us
    gather x1, local copies, waits for them, and re-layouts, return_slots(): return pad_rows(results)[row_index]  12.9 us
    reduce_sum x1, other arithmetic, body(): jnp.sum(lax.all_gather(both_parts.astype(jnp.bfloat16), 'expert'), axis=0)  9.15 us
    gather x1, local copies, waits for them, and re-layouts, body(): returned.reshape(experts * slot_count, feat_width)  8.78 us
    scatter x1, local copies, waits for them, and re-layouts, body(): pack_index = jnp.full((local_experts * capacity,), all_rows, jnp.int32).a...  8.04 us
  transfers between devices with their start and end apart: 3, of which 3 were waited for; matrix products, arithmetic and copies ran while one was open for 8% of the time, Pallas kernels for 0%

profile of v1, /device:TPU:0, one launch (start us, length us, event | category | flops | bytes accessed | tf_op | source)
XLA Modules:
  0.0 369.5 jit_solution(14124152021767163328)
XLA Ops:
  7.2 0.0 copy-start
  7.2 0.0 all-gather.3.cloned.1.call-start
  7.2 0.7 all-gather.3.cloned.1.call-update
  7.9 0.0 all-gather.5.cloned.1.call-start
  8.0 6.4 %all_gather.10 = s32[512,8]{0,1:T(8,128)S(1)} all-gather(s32[128,8]{0,1:T(8,128)} %param.13), channel_id=1, replica_groups=mesh['groups'=2,'attn'=4,'expert'=4] {'attn'}, dimensions={0}, use_global_device_ids=true | all-gather | bytes 20480 | tf_op jit(solution)/shard_map/all_gather | solution.py:63
  14.5 1.2 reduce-window.6
  15.7 0.2 slice_reduce_fusion
  15.9 0.2 reduce-window.9
  16.1 0.1 add_bitcast_fusion
  16.2 0.1 add_select_fusion
  16.2 0.1 copy.124
  16.4 0.2 reshape.169
  16.6 0.2 reshape.217
  16.8 8.0 %scatter_custom_fusion = s32[1024]{0:T(1024)S(1)} fusion(s32[2048]{0:T(1024)S(1)} %bitcast.60, s32[2048]{0:T(1024)S(1)} %reshape.217, s32[]{:T(128)} %constant.34.clone.1), kind=kCustom, calls=%fused_computation.59 | custom fusion | bytes 4100 | tf_op jit(solution)/shard_map/scatter | solution.py:91
  24.9 4.2 %all-gather.3.cloned.1.call-done = bf16[512,1024]{1,0:T(8,128)(2,1)} async-done(((bf16[128,1024]{1,0:T(8,128)(2,1)}), bf16[512,1024]{1,0:T(8,128)(2,1)}) %all-gather.3.cloned.1.call-update) | async-done | bytes 1048592 | tf_op jit(solution)/shard_map/all_gather | solution.py:62
  29.0 1.3 concatenate.21
  30.3 5.4 %gather_fusion = bf16[1024,1024]{1,0:T(8,128)(2,1)} fusion(bf16[513,1024]{1,0:T(8,128)(2,1)S(1)} %concatenate.21, s32[1024]{0:T(1024)S(1)} %fusion.26), kind=kCustom, calls=%fused_computation.2 | custom fusion | bytes 4198400 | tf_op jit(solution)/shard_map/gather | solution.py:93
  35.7 0.0 copy-start.1
  35.7 5.4 %fusion.10 = bf16[1,4,256,768]{3,2,1,0:T(8,128)(2,1)S(1)} fusion(bf16[4,256,1024]{2,1,0:T(8,128)(2,1)} %bitcast.52, bf16[4,1024,768]{2,1,0:T(8,128)(2,1)} %param.16), kind=kOutput, calls=%fused_computation.21 | convolution fusion | flops 1611399168 | bytes 9961472 | tf_op jit(solution)/shard_map/jrd,jdf->jrf/dot_general | solution.py:95
  41.0 0.0 copy-done.1
  41.0 4.6 %fusion.9 = bf16[1,4,256,768]{3,2,1,0:T(8,128)(2,1)S(1)} fusion(bf16[4,256,1024]{2,1,0:T(8,128)(2,1)S(1)} %bitcast.53, bf16[4,1024,768]{2,1,0:T(8,128)(2,1)} %param.15), kind=kOutput, calls=%fused_computation.20 | convolution fusion | flops 1611399168 | bytes 9961472 | tf_op jit(solution)/shard_map/jrd,jdf->jrf/dot_general | solution.py:94
  45.6 1.9 pad_maximum_fusion
  47.6 0.0 all-gather.5.cloned.1.call-update
  47.6 0.3 reduce_sum.39
  48.0 0.2 reduce_window_sum.37
  48.1 0.1 dynamic-slice_minimum_fusion
  48.2 0.1 copy.125
  48.3 0.1 copy.126
  48.4 0.1 compare_select_fusion.1
  48.5 217.5 %all-gather.5.cloned.1.call-done = bf16[4,4,256,1536]{3,2,1,0:T(8,128)(2,1)} async-done(((bf16[1,4,256,1536]{3,2,1,0:T(8,128)(2,1)}), bf16[4,4,256,1536]{3,2,1,0:T(8,128)(2,1)}) %all-gather.5.cloned.1.call-update) | async-done | bytes 12582928 | tf_op jit(solution)/shard_map/all_gather | solution.py:97
  265.9 9.2 %reduce_sum.40 = bf16[4,256,1536]{2,1,0:T(8,128)(2,1)} reduce(bf16[4,4,256,1536]{3,2,1,0:T(8,128)(2,1)} %all-gather.5.cloned.1.call-done, bf16[]{:T(256)} %constant.19.clone.1), dimensions={0}, to_apply=%region_8.10 | reduce | flops 4718592 | bytes 15728642 | tf_op jit(solution)/shard_map/reduce_sum | solution.py:97
  275.1 2.7 convert_element_type.54
  277.8 4.8 %convolution_convert_fusion = bf16[4,256,1024]{2,1,0:T(8,128)(2,1)S(1)} fusion(bf16[4,768,1024]{2,1,0:T(8,128)(2,1)} %param.17, f32[4,256,1536]{2,1,0:T(8,128)S(1)} %convert_element_type.54), kind=kOutput, calls=%fused_computation.12 | convolution fusion | flops 1616379904 | bytes 14680064 | tf_op jit(solution)/shard_map/jrf,jfd->jrd/dot_general | solution.py:103
  282.7 1.5 concatenate.25
  284.2 12.9 %gather_fusion.1 = bf16[2048,1024]{1,0:T(8,128)(2,1)} fusion(bf16[1025,1024]{1,0:T(8,128)(2,1)} %concatenate.25, s32[2048]{0:T(1024)S(1)} %broadcast_clamp_fusion), kind=kCustom, calls=%fused_computation.3 | custom fusion | bytes 8396800 | tf_op jit(solution)/shard_map/gather | solution.py:25
  297.1 5.2 %all-to-all-start = ((bf16[4,4,128,1024]{3,2,1,0:T(8,128)(2,1)}), bf16[4,4,128,1024]{3,2,1,0:T(8,128)(2,1)}, u32[]{:S(2)}, u32[]{:S(2)}) async-start(bf16[4,4,128,1024]{3,2,1,0:T(8,128)(2,1)} %bitcast.51), calls=%async_computation | async-start | bytes 8388608 | tf_op jit(solution)/shard_map/all_to_all | solution.py:107
  302.2 0.0 copy-done.2
  302.3 0.1 copy.120
  302.4 0.2 reduce_window_sum.38
  302.6 0.1 copy.121
  302.7 0.1 reshape.237
  302.8 0.2 dynamic-slice_reduce_fusion
  303.0 7.1 %gather_fusion.4 = s32[1024]{0:T(1024)S(1)} fusion(s32[128,16]{1,0:T(8,128)S(1)} %get-tuple-element.4, s32[1024]{0:T(1024)S(1)} %reshape.237), kind=kCustom, calls=%fused_computation.1.clone | custom fusion | bytes 16384 | tf_op jit(solution)/shard_map/jit(take_along_axis)/gather | solution.py:108
  310.1 0.1 reshape.245
  310.2 0.1 copy.129
  310.4 0.1 reshape.207
  310.5 0.0 copy-start.4
  310.5 0.0 copy-start.5
  310.5 0.0 copy-start.3
  310.5 7.1 %gather_fusion.3 = s32[1024]{0:T(1024)S(1)} fusion(s32[128,16]{1,0:T(8,128)S(1)} %get-tuple-element.3, s32[1024]{0:T(1024)S(1)} %reshape.237), kind=kCustom, calls=%fused_computation.clone | custom fusion | bytes 16384 | tf_op jit(solution)/shard_map/jit(take_along_axis)/gather | solution.py:109
  317.6 0.1 reshape.240
  317.7 0.0 copy-done.4
  317.7 0.1 copy.123
  317.8 0.0 copy-done.5
  317.8 0.1 iota_compare_fusion.3
  317.9 0.0 copy-done
  317.9 0.0 copy-done.3
  317.9 0.5 fusion.16
  318.4 0.2 fusion.31
  318.7 1.8 fusion.19
  320.5 0.7 copy.148
  321.2 29.1 %all-to-all-done = bf16[4,4,128,1024]{3,2,1,0:T(8,128)(2,1)} async-done(((bf16[4,4,128,1024]{3,2,1,0:T(8,128)(2,1)}), bf16[4,4,128,1024]{3,2,1,0:T(8,128)(2,1)}, u32[]{:S(2)}, u32[]{:S(2)}) %all-to-all-start) | async-done | bytes 4194336 | tf_op jit(solution)/shard_map/all_to_all | solution.py:107
  350.3 8.8 %gather_fusion.2 = bf16[1024,1024]{1,0:T(8,128)(2,1)} fusion(bf16[2048,1024]{1,0:T(8,128)(2,1)} %bitcast.10, s32[1024]{0:T(1024)S(1)} %broadcast_clamp_fusion.1), kind=kCustom, calls=%fused_computation.4 | custom fusion | bytes 4198400 | tf_op jit(solution)/shard_map/gather | solution.py:111
  359.0 3.7 fusion.1
  (21 shorter events, 0.3 us)
Async XLA Ops:
  7.2 310.8 %copy-start = (bf16[2,768,4,128]{3,2,1,0:T(4,128)(2,1)S(1)}, bf16[2,768,4,128]{3,2,1,0:T(4,128)(2,1)}, u32[]{:S(2)}) copy-start(bf16[2,768,4,128]{3,2,1,0:T(4,128)(2,1)} %param.19) | copy-start | bytes 4718596
  7.2 21.8 %all-gather.3.cloned.1.call-start = ((), (), s32[]{:S(2)}) async-start(), calls=%async_computation.1 | async-start | bytes 1310720 | tf_op jit(solution)/shard_map/all_gather | solution.py:62
  7.9 258.0 %all-gather.5.cloned.1.call-start = ((), (), s32[]{:S(2)}) async-start(), calls=%async_computation.2 | async-start | bytes 15728640 | tf_op jit(solution)/shard_map/all_gather | solution.py:97
  35.7 5.4 %copy-start.1 = (bf16[1024,1024]{1,0:T(8,128)(2,1)S(1)}, bf16[1024,1024]{1,0:T(8,128)(2,1)}, u32[]{:S(2)}) copy-start(bf16[1024,1024]{1,0:T(8,128)(2,1)} %gather_fusion) | copy-start | bytes 6291460
  297.1 5.2 %copy-start.2 = (s32[128,8]{0,1:T(8,128)S(1)}, s32[128,8]{0,1:T(8,128)}, u32[]{:S(2)}) copy-start(s32[128,8]{0,1:T(8,128)} %param.13) | copy-start | bytes 12292
  297.1 53.2 %all-to-all-start = ((bf16[4,4,128,1024]{3,2,1,0:T(8,128)(2,1)}), bf16[4,4,128,1024]{3,2,1,0:T(8,128)(2,1)}, u32[]{:S(2)}, u32[]{:S(2)}) async-start(bf16[4,4,128,1024]{3,2,1,0:T(8,128)(2,1)} %bitcast.51), calls=%async_computation | async-start | bytes 8388608 | tf_op jit(solution)/shard_map/all_to_all | solution.py:107
  310.5 7.3 %copy-start.4 = (bf16[128,8]{0,1:T(8,128)(2,1)S(1)}, bf16[128,8]{0,1:T(8,128)(2,1)}, u32[]{:S(2)}) copy-start(bf16[128,8]{0,1:T(8,128)(2,1)} %param.14) | copy-start | bytes 6148
  310.5 7.4 %copy-start.5 = (s32[2]{0:T(128)S(1)}, s32[2]{0:T(128)}, u32[]{:S(2)}) copy-start(s32[2]{0:T(128)} %param.21) | copy-start | bytes 28
  310.5 7.4 %copy-start.3 = (bf16[2,64,128]{2,1,0:T(8,128)(2,1)S(1)}, bf16[2,64,128]{2,1,0:T(8,128)(2,1)}, u32[]{:S(2)}) copy-start(bf16[2,64,128]{2,1,0:T(8,128)(2,1)} %param.18) | copy-start | bytes 98308
Sparse Core Ops, SparseCore 0:
  9.5 19.4 all-gather.2
  47.7 218.1 all-gather.4
